TPU v7x, 32 devices: a whole 2x2x4 slice. The times are simulated.
32 devices in a mesh: leaf: 32 (over z, y, x, core).
Axes of the slice: x: 2, y: 2, z: 4, core: 2. Of those that a mesh axis runs over, the one named last changes fastest.
Arguments:
- coords: float32 [3, 262144], P(None, 'leaf'), may hold values from 0 to 1
- charges: bfloat16 [262144, 128], P('leaf'), may hold values from -6 to 6
- near_leaves: int32 [2048, 27], P('leaf'), may hold values from 0 to 191
- leaf_basis: bfloat16 [2048, 4096], P('leaf'), may hold values from -1 to 1
- leaf_transfer: bfloat16 [2048, 1024], P('leaf'), may hold values from -0.75 to 0.75
- mid_transfer: bfloat16 [256, 1024], P('leaf'), may hold values from -0.75 to 0.75
- base_transfer: bfloat16 [32, 1024], P('leaf'), may hold values from -0.75 to 0.75
- base_coupling: bfloat16 [6048, 1024], P('leaf'), may hold values from -0.01953125 to 0.01953125
- base_target: int32 [6048, 1], P('leaf'), may hold values from 0 to 31; in each aligned block of 189 rows (0 to 188, 189 to 377, ...) at most 11 rows name the same one
- base_source: int32 [6048], P('leaf'), may hold values from 0 to 31
- top_coupling: bfloat16 [256, 1024], P('leaf'), may hold values from -0.015625 to 0.015625
- top_target: int32 [256], P('leaf'), may hold values from 0 to 3
- top_source: int32 [256], P('leaf'), may hold values from 0 to 3
Outputs:
- potential: bfloat16 [262144, 128], P('leaf')
Inputs may be any that keep to these rules, and one draw needn't show every extreme that they name: `near_leaves`: entry j of leaf l names leaf 64 * (l // 64 - 1) + j: a leaf of the device before in Morton order, of the row's own device, or of the device after; repeats may occur. `base_target`: among the 189 blocks of one device no base cluster is the target more than 11 times; that count is reached.
All inputs are finite; a program needn't handle non-finite values.
Results may differ from a plain program's by a relative error of at most 0.01.
Values may be sent and summed in bfloat16 or wider, within the bound.
A program may use at most 128 MiB of HBM per device.

v0:
```python
import math
import jax
import jax.numpy as jnp
from jax import lax
from jax.sharding import PartitionSpec as P

K = 32
RHS = 128
M = 128
NB = 189
delta_sq = 0.0025


def extended(array, sides, width):
    for axis, dim in sides:
        size, length = (lax.axis_size(axis), array.shape[dim])
        up = [(i, (i + 1) % size) for i in range(size - 1)]
        down = [(j, i) for i, j in up]
        last = lax.slice_in_dim(array, length - width, length, axis=dim)
        first = lax.slice_in_dim(array, 0, width, axis=dim)
        before = lax.ppermute(last, axis, up)
        after = lax.ppermute(first, axis, down)
        array = jnp.concatenate([before, array, after], axis=dim)
    return array


def near_block(points, pool_points, pool_charges, columns):
    near_scale = 1.0 / math.sqrt(columns.shape[1] * points.shape[2])

    def near_step(running, column):
        other_points = jnp.take(pool_points, column, axis=1)
        other_charges = jnp.take(pool_charges, column, axis=0)
        squares = jnp.sum((points[:, :, :, None] - other_points[:, :, None, :]) ** 2, axis=0)
        kernel = (near_scale / jnp.sqrt(squares + delta_sq)).astype(jnp.bfloat16)
        update = jnp.einsum(
            "lab,lbr->lar", kernel, other_charges, preferred_element_type=jnp.float32
        )
        return (running + update, None)

    initial = jnp.zeros((points.shape[1], points.shape[2], pool_charges.shape[2]), jnp.float32)
    running, unused = lax.scan(near_step, initial, columns.T)
    return running


def per_device(
    coords,
    charges,
    near_leaves,
    leaf_basis,
    leaf_transfer,
    mid_transfer,
    base_transfer,
    base_coupling,
    base_target,
    base_source,
    top_coupling,
    top_target,
    top_source,
):
    single_precision = jnp.float32
    bf16 = jnp.bfloat16
    leaves = leaf_basis.shape[0]
    mid_count = leaves // 8
    base_count = leaves // 64
    devices = lax.axis_size("leaf")
    position = lax.axis_index("leaf")
    charge_row_block = charges.reshape(leaves, M, RHS)
    own_points = coords.reshape(3, leaves, M)
    point_rows = own_points.transpose(1, 0, 2).reshape(leaves, 3 * M)
    pool_points = (
        extended(point_rows, (("leaf", 0),), leaves).reshape(3 * leaves, 3, M).transpose(1, 0, 2)
    )
    pool_charges = extended(
        charge_row_block.reshape(leaves, M * RHS), (("leaf", 0),), leaves
    ).reshape(3 * leaves, M, RHS)
    basis_matrix = leaf_basis.reshape(leaves, K, M)
    leaf_coefficients = jnp.einsum(
        "xpt,xtu->xpu", basis_matrix, charge_row_block, preferred_element_type=single_precision
    ).astype(bf16)
    mid_coeffs = jnp.einsum(
        "mckp,mckr->mpr",
        leaf_transfer.reshape(mid_count, 8, K, K),
        leaf_coefficients.reshape(mid_count, 8, K, RHS),
        preferred_element_type=single_precision,
    ).astype(bf16)
    base_coeffs = jnp.einsum(
        "mckp,mckr->mpr",
        mid_transfer.reshape(base_count, 8, K, K),
        mid_coeffs.reshape(base_count, 8, K, RHS),
        preferred_element_type=single_precision,
    ).astype(bf16)
    base_lift = base_transfer.reshape(base_count, K, K)
    lifted = jnp.einsum(
        "bkp,bkr->bpr", base_lift, base_coeffs, preferred_element_type=single_precision
    ).astype(bf16)
    all_coeffs, all_lifted = (
        lax.all_gather(base_coeffs.reshape(base_count, K * RHS), "leaf", axis=0, tiled=True),
        lax.all_gather(lifted.reshape(base_count, K * RHS), "leaf", axis=0, tiled=True),
    )
    total_bases = base_count * devices
    total_tops = total_bases // 8
    every_base = all_coeffs.reshape(total_bases, K, RHS)
    top_coeffs = jnp.sum(
        all_lifted.reshape(total_tops, 8, K, RHS).astype(single_precision), axis=1
    ).astype(bf16)
    top_products = jnp.einsum(
        "bts,bsr->btr",
        top_coupling.reshape(-1, K, K),
        jnp.take(top_coeffs, top_source, axis=0),
        preferred_element_type=single_precision,
    )
    top_partial = jax.ops.segment_sum(top_products, top_target, num_segments=total_tops)
    top_sum = lax.psum(top_partial, "leaf")
    top_field = top_sum.astype(bf16)
    targets = base_target[:, 0]
    per_cluster = max(2, 2 * NB // devices)
    per_owner = per_cluster * base_count
    owners = targets // base_count
    onehot = (owners[:, None] == jnp.arange(devices, dtype=jnp.int32)[None, :]).astype(jnp.int32)
    earlier = jnp.cumsum(onehot, axis=0) - onehot
    slot_index = jnp.sum(earlier * onehot, axis=1)
    placed = owners * per_owner + slot_index
    send_blocks = jnp.zeros((devices * per_owner, K * K), bf16).at[placed].set(base_coupling)
    labels = base_source * base_count + (targets - owners * base_count)
    send_labels = jnp.full((devices * per_owner,), -1, jnp.int32).at[placed].set(labels)
    sent = (send_blocks.reshape(devices, per_owner, K * K), send_labels.reshape(devices, per_owner))
    blocks = lax.all_to_all(sent[0], "leaf", split_axis=0, concat_axis=0, tiled=True)
    got_labels = lax.all_to_all(sent[1], "leaf", split_axis=0, concat_axis=0, tiled=True)
    present = got_labels >= 0
    source_ids = jnp.where(present, got_labels // base_count, 0)
    gathered = jnp.take(every_base, source_ids, axis=0)
    shaped = blocks.reshape(blocks.shape[0], blocks.shape[1], K, K)
    result = jnp.einsum(
        "dnts,dnsr->dntr", shaped, gathered, preferred_element_type=single_precision
    )
    results, got_labels = (result, got_labels)
    local_ids = jnp.where(got_labels >= 0, got_labels % base_count, base_count).reshape(-1)
    coupled = jax.ops.segment_sum(results.reshape(-1, K, RHS), local_ids, num_segments=base_count)
    my_bases = position * base_count + jnp.arange(base_count, dtype=jnp.int32)
    top_mine = jnp.take(top_field, my_bases // 8, axis=0)
    base_field = (
        coupled
        + jnp.einsum("bkp,bpr->bkr", base_lift, top_mine, preferred_element_type=single_precision)
    ).astype(bf16)
    mid_field = jnp.einsum(
        "mkp,mpr->mkr",
        mid_transfer.reshape(mid_count, K, K),
        jnp.repeat(base_field, 8, axis=0),
        preferred_element_type=single_precision,
    ).astype(bf16)
    leaf_potential = jnp.einsum(
        "lkp,lpr->lkr",
        leaf_transfer.reshape(leaves, K, K),
        jnp.repeat(mid_field, 8, axis=0),
        preferred_element_type=single_precision,
    ).astype(bf16)
    near_field = near_block(own_points, pool_points, pool_charges, near_leaves)
    distant_field = jnp.einsum(
        "cbz,cbw->czw", basis_matrix, leaf_potential, preferred_element_type=single_precision
    )
    return (near_field + distant_field).astype(bf16).reshape(leaves * M, RHS)


def solution(mesh):
    in_specs = (
        P(None, "leaf"),
        P("leaf", None),
        P("leaf", None),
        P("leaf", None),
        P("leaf", None),
        P("leaf", None),
        P("leaf", None),
        P("leaf", None),
        P("leaf", None),
        P("leaf"),
        P("leaf", None),
        P("leaf"),
        P("leaf"),
    )
    out_specs = P("leaf", None)
    return jax.shard_map(
        per_device, mesh=mesh, in_specs=in_specs, out_specs=out_specs, check_vma=False
    )
```

profile of v0, /device:TPU:0, one launch (start us, length us, event | category | flops | bytes accessed | tf_op | source)
XLA Modules:
  0.0 797.9 jit_solution(6871703731802868991)
XLA Ops:
  12.2 5.8 collective-permute-start.2
  21.0 8.4 %all-to-all-start = ((s32[32,1,11]{2,1,0:T(1,128)}), s32[32,1,11]{2,1,0:T(1,128)S(1)}, u32[]{:S(2)}, u32[]{:S(2)}) async-start(s32[32,1,11]{2,1,0:T(1,128)} %bitcast.22), calls=%async_computation | async-start | bytes 32768 | tf_op jit(solution)/shard_map/all_to_all | solution.py:128
  33.9 64.6 %all-gather = bf16[32,1,4096]{2,1,0:T(2,128)(2,1)S(1)} all-gather(bf16[1,1,4096]{2,1,0:T(2,128)(2,1)S(1)} %reshape.358), channel_id=1, replica_groups=mesh['leaf'=32] {'leaf'}, dimensions={0}, use_global_device_ids=true | all-gather | bytes 270336 | tf_op jit(solution)/shard_map/all_gather | solution.py:98
  102.0 38.0 %all-gather.1 = bf16[32,1,4096]{2,1,0:T(2,128)(2,1)S(1)} all-gather(bf16[1,1,4096]{2,1,0:T(2,128)(2,1)S(1)} %reshape.360), channel_id=1, replica_groups=mesh['leaf'=32] {'leaf'}, dimensions={0}, use_global_device_ids=true | all-gather | bytes 270336 | tf_op jit(solution)/shard_map/all_gather | solution.py:97
  158.2 40.9 %psum.7 = bf16[4,32,128]{2,1,0:T(8,128)(2,1)S(1)} all-reduce(f32[4,32,128]{2,1,0:T(8,128)S(1)} %scatter_fusion), channel_id=1, replica_groups=mesh['leaf'=32] {'leaf'}, use_global_device_ids=true, to_apply=%region_5.6 | all-reduce | flops 16384 | bytes 98304 | tf_op jit(solution)/shard_map/psum | solution.py:113
  208.3 4.7 reshape.373
  213.0 6.1 fusion.10
  219.1 31.1 %scatter_fusion.1 = f32[32,128,1]{1,0,2:T(8,128)S(1)} fusion(f32[32,128,1]{1,0,2:T(8,128)S(1)} %convolution_bitcast_fusion.2, s32[352]{0:T(512)S(1)} %reshape.354, f32[352,32,128]{2,1,0:T(8,128)} %bitcast.136), kind=kCustom, calls=%fused_computation.7 | custom fusion | flops 1441792 | bytes 17302912 | tf_op jit(solution)/shard_map/scatter-add | solution.py:138
  255.4 5.1 pad_maximum_fusion
  260.5 532.9 %while.12 = (s32[]{:T(128)}, f32[64,128,128]{2,1,0:T(8,128)}, f32[3,8192]{1,0:T(4,128)S(1)}, s32[27,64]{1,0:T(8,128)}, f32[3,192,128]{2,0,1:T(4,128)}, /*index=5*/bf16[192,128,128]{2,1,0:T(8,128)(2,1)}, s32[]{:T(128)}, s32[]{:T(128)}) while((s32[]{:T(128)}, f32[64,128,128]{2,1,0:T(8,128)}, f32[3,8192]{1,0:T(4,128)S(1)}, ...), condition=%wide.region_2.3_spmd.clone, body=%wide.region_0.2_spmd.clone.sunk | while | flops 283141696 | bytes 24057648 | solution.py:41
  263.8 6.2 multiply_reduce_fusion.2
  273.7 5.3 select_add_fusion.2
  282.3 6.2 multiply_reduce_fusion.2
  292.2 6.6 select_add_fusion.2
  302.1 6.2 multiply_reduce_fusion.2
  312.0 6.6 select_add_fusion.2
  321.8 6.2 multiply_reduce_fusion.2
  331.8 6.6 select_add_fusion.2
  341.6 6.2 multiply_reduce_fusion.2
  351.6 6.6 select_add_fusion.2
  361.4 6.2 multiply_reduce_fusion.2
  371.4 6.6 select_add_fusion.2
  381.2 6.2 multiply_reduce_fusion.2
  391.2 6.6 select_add_fusion.2
  401.0 6.2 multiply_reduce_fusion.2
  410.9 6.6 select_add_fusion.2
  420.8 6.2 multiply_reduce_fusion.2
  430.7 6.6 select_add_fusion.2
  440.5 6.2 multiply_reduce_fusion.2
  450.5 6.6 select_add_fusion.2
  460.3 6.2 multiply_reduce_fusion.2
  470.3 6.6 select_add_fusion.2
  480.1 6.2 multiply_reduce_fusion.2
  490.1 6.6 select_add_fusion.2
  499.9 6.2 multiply_reduce_fusion.2
  509.8 6.6 select_add_fusion.2
  519.7 6.2 multiply_reduce_fusion.2
  529.6 6.6 select_add_fusion.2
  539.5 6.2 multiply_reduce_fusion.2
  549.4 6.6 select_add_fusion.2
  559.2 6.2 multiply_reduce_fusion.2
  569.2 6.6 select_add_fusion.2
  579.0 6.2 multiply_reduce_fusion.2
  589.0 6.6 select_add_fusion.2
  598.8 6.2 multiply_reduce_fusion.2
  608.8 6.6 select_add_fusion.2
  618.6 6.2 multiply_reduce_fusion.2
  628.5 6.6 select_add_fusion.2
  638.4 6.2 multiply_reduce_fusion.2
  648.3 6.6 select_add_fusion.2
  658.1 6.2 multiply_reduce_fusion.2
  668.1 6.6 select_add_fusion.2
  677.9 6.2 multiply_reduce_fusion.2
  687.9 6.6 select_add_fusion.2
  697.7 6.2 multiply_reduce_fusion.2
  707.7 6.6 select_add_fusion.2
  717.5 6.2 multiply_reduce_fusion.2
  727.5 6.6 select_add_fusion.2
  737.3 6.2 multiply_reduce_fusion.2
  747.2 6.6 select_add_fusion.2
  757.1 6.2 multiply_reduce_fusion.2
  767.0 6.6 select_add_fusion.2
  776.8 6.2 multiply_reduce_fusion.2
  786.8 6.6 select_add_fusion.2
  (315 shorter events, 247.1 us)
Async XLA Ops:
  0.0 18.0 %copy-start.13 = (s32[189,1]{0,1:T(1,128)S(1)}, s32[189,1]{0,1:T(1,128)}, u32[]{:S(2)}) copy-start(s32[189,1]{0,1:T(1,128)} %param.23) | copy-start | bytes 2272
  0.0 29.5 %copy-start.7 = (bf16[64,4096]{1,0:T(8,128)(2,1)S(1)}, bf16[64,4096]{1,0:T(8,128)(2,1)}, u32[]{:S(2)}) copy-start(bf16[64,4096]{1,0:T(8,128)(2,1)} %param.18) | copy-start | bytes 1572868
  0.0 29.6 %copy-start.12 = (bf16[8,1024]{1,0:T(8,128)(2,1)S(1)}, bf16[8,1024]{1,0:T(8,128)(2,1)}, u32[]{:S(2)}) copy-start(bf16[8,1024]{1,0:T(8,128)(2,1)} %param.20) | copy-start | bytes 49156
  0.0 29.7 %copy-start.14 = (bf16[1,1024]{1,0:T(2,128)(2,1)S(1)}, bf16[1,1024]{1,0:T(2,128)(2,1)}, u32[]{:S(2)}) copy-start(bf16[1,1024]{1,0:T(2,128)(2,1)} %param.21) | copy-start | bytes 6148
  1.6 28.2 %copy-start.5 = (bf16[64,1024]{1,0:T(8,128)(2,1)S(1)}, bf16[64,1024]{1,0:T(8,128)(2,1)}, u32[]{:S(2)}) copy-start(bf16[64,1024]{1,0:T(8,128)(2,1)} %param.19) | copy-start | bytes 393220
  1.6 28.6 %copy-start = (bf16[8192,128]{1,0:T(8,128)(2,1)S(1)}, bf16[8192,128]{1,0:T(8,128)(2,1)}, u32[]{:S(2)}) copy-start(bf16[8192,128]{1,0:T(8,128)(2,1)} %param.16) | copy-start | bytes 6291460
  1.6 203.9 %collective-permute-start.1 = (f32[64,384]{1,0:T(8,128)}, f32[64,384]{1,0:T(8,128)}, u32[]{:S(2)}, u32[]{:S(2)}) collective-permute-start(f32[64,384]{1,0:T(8,128)} %bitcast.122), channel_id=1, source_target_pairs={{1,0},{2,1},{3,2},{4,3},{5,4},{6,5},{7,6},{8,7},{9,8},{10,9},{11,1... | collective-permute-start | bytes 294920 | tf_op jit(solution)/shard_map/ppermute | solution.py:22
  3.0 203.5 %collective-permute-start = (f32[64,384]{1,0:T(8,128)}, f32[64,384]{1,0:T(8,128)}, u32[]{:S(2)}, u32[]{:S(2)}) collective-permute-start(f32[64,384]{1,0:T(8,128)} %bitcast.122), channel_id=1, source_target_pairs={{0,1},{1,2},{2,3},{3,4},{4,5},{5,6},{6,7},{7,8},{8,9},{9,10},{10,1... | collective-permute-start | bytes 294920 | tf_op jit(solution)/shard_map/ppermute | solution.py:21
  10.9 240.1 %collective-permute-start.3 = (bf16[64,16384]{1,0:T(8,128)(2,1)}, bf16[64,16384]{1,0:T(8,128)(2,1)}, u32[]{:S(2)}, u32[]{:S(2)}) collective-permute-start(bf16[64,16384]{1,0:T(8,128)(2,1)} %reshape_reshape.3), channel_id=1, source_target_pairs={{1,0},{2,1},{3,2},{4,3},{5,4},{6,5},{7,6},{8,7},{9,8},{10,9},{11,1... | collective-permute-start | bytes 6291464 | tf_op jit(solution)/shard_map/ppermute | solution.py:22
  12.2 241.0 %collective-permute-start.2 = (bf16[64,16384]{1,0:T(8,128)(2,1)}, bf16[64,16384]{1,0:T(8,128)(2,1)}, u32[]{:S(2)}, u32[]{:S(2)}) collective-permute-start(bf16[64,16384]{1,0:T(8,128)(2,1)} %reshape_reshape.3), channel_id=1, source_target_pairs={{0,1},{1,2},{2,3},{3,4},{4,5},{5,6},{6,7},{7,8},{8,9},{9,10},{10,1... | collective-permute-start | bytes 6291464 | tf_op jit(solution)/shard_map/ppermute | solution.py:21
  19.0 14.2 %copy-start.15 = (s32[189,1]{0,1:T(1,128)}, s32[189,1]{0,1:T(1,128)S(1)}, u32[]{:S(2)}) copy-start(s32[189,1]{0,1:T(1,128)S(1)} %compare_select_fusion.7) | copy-start | bytes 2272
  21.0 124.0 %all-to-all-start = ((s32[32,1,11]{2,1,0:T(1,128)}), s32[32,1,11]{2,1,0:T(1,128)S(1)}, u32[]{:S(2)}, u32[]{:S(2)}) async-start(s32[32,1,11]{2,1,0:T(1,128)} %bitcast.22), calls=%async_computation | async-start | bytes 32768 | tf_op jit(solution)/shard_map/all_to_all | solution.py:128
  29.7 70.3 %copy-start.3 = (bf16[8,32,32]{2,1,0:T(8,128)(2,1)}, bf16[8,32,32]{2,1,0:T(8,128)(2,1)S(1)}, u32[]{:S(2)}) copy-start(bf16[8,32,32]{2,1,0:T(8,128)(2,1)S(1)} %reshape.231) | copy-start | bytes 49156
  29.8 3.3 copy-start.11
  33.1 0.6 copy-start.10
  100.0 49.0 %copy-start.6 = (bf16[64,1024]{1,0:T(8,128)(2,1)S(1)}, bf16[64,1024]{1,0:T(8,128)(2,1)}, u32[]{:S(2)}) copy-start(bf16[64,1024]{1,0:T(8,128)(2,1)} %param.19) | copy-start | bytes 393220
  145.1 8.8 %copy-start.9 = (s32[32,1,11]{2,1,0:T(1,128)}, s32[32,1,11]{2,1,0:T(1,128)S(1)}, u32[]{:S(2)}) copy-start(s32[32,1,11]{2,1,0:T(1,128)S(1)} %all-to-all-done) | copy-start | bytes 4228
  145.1 63.2 %all-to-all-start.1 = ((bf16[32,11,1024]{2,1,0:T(8,128)(2,1)}), bf16[32,11,1024]{2,1,0:T(8,128)(2,1)}, u32[]{:S(2)}, u32[]{:S(2)}) async-start(bf16[32,11,1024]{2,1,0:T(8,128)(2,1)} %reshape.239), calls=%async_computation.1 | async-start | bytes 2097152 | tf_op jit(solution)/shard_map/all_to_all | solution.py:127
  202.4 5.0 copy-start.1
  219.1 31.1 %copy-start.4 = (bf16[8,32,32]{2,1,0:T(8,128)(2,1)S(1)}, bf16[8,32,32]{2,1,0:T(8,128)(2,1)}, u32[]{:S(2)}) copy-start(bf16[8,32,32]{2,1,0:T(8,128)(2,1)} %copy-done.3) | copy-start | bytes 49156
  260.5 532.9 %copy-start.8 = (bf16[8,32,128]{2,1,0:T(8,128)(2,1)S(1)}, bf16[8,32,128]{2,1,0:T(8,128)(2,1)}, u32[]{:S(2)}) copy-start(bf16[8,32,128]{2,1,0:T(8,128)(2,1)} %fusion.15) | copy-start | bytes 196612
  260.5 533.0 %copy-start.2 = (bf16[64,32,32]{2,1,0:T(8,128)(2,1)S(1)}, bf16[64,32,32]{2,1,0:T(8,128)(2,1)}, u32[]{:S(2)}) copy-start(bf16[64,32,32]{2,1,0:T(8,128)(2,1)} %copy.43) | copy-start | bytes 393220
where the time goes:
time: 804 us; the launch traced here: 798 us
  other arithmetic  257 us (32%)
  matrix products  192 us (24%)
  local copies, waits for them, and re-layouts  180 us (22%)
  blocking collectives  144 us (18%)
  starting transfers between devices  24 us (3%)
    dot_general x27, matrix products, near_step(): jnp.einsum('lab,lbr->lar', kernel, other_charges, preferred_element_type=...  176 us
    reduce_sum x27, other arithmetic, near_step(): jnp.sum((points[:, :, :, None] - other_points[:, :, None, :]) ** 2, axis=0)  168 us
    gather x27, local copies, waits for them, and re-layouts, near_step(): other_charges = jnp.take(pool_charges, column, axis=0)  101 us
    all_gather x1, blocking collectives, per_device(): lax.all_gather(lifted.reshape(base_count, K * RHS), 'leaf', axis=0, tiled...  64.6 us
    gather x27, local copies, waits for them, and re-layouts, near_step(): other_points = jnp.take(pool_points, column, axis=1)  44.5 us
    psum x1, blocking collectives, per_device(): top_sum = lax.psum(top_partial, 'leaf')  40.9 us
    all_gather x1, blocking collectives, per_device(): lax.all_gather(base_coeffs.reshape(base_count, K * RHS), 'leaf', axis=0,...  38 us
    scatter-add x1, other arithmetic, per_device(): jax.ops.segment_sum(results.reshape(-1, K, RHS), local_ids, num_segments=...  31.1 us
  transfers between devices with their start and end apart: 6, of which 0 were waited for; matrix products, arithmetic and copies ran while one was open for 10% of the time, Pallas kernels for 0%

commit v1 on v0

--- a/solution.py
+++ b/solution.py
@@ -110,7 +110,7 @@
         preferred_element_type=single_precision,
     )
     top_partial = jax.ops.segment_sum(top_products, top_target, num_segments=total_tops)
-    top_sum = lax.psum(top_partial, "leaf")
+    top_sum = jnp.sum(lax.all_gather(top_partial, "leaf"), axis=0)
     top_field = top_sum.astype(bf16)
     targets = base_target[:, 0]
     per_cluster = max(2, 2 * NB // devices)

time: 804 us -> 748 us (0.930)
  local copies, waits for them, and re-layouts: 180 us -> 151 us
  blocking collectives: 144 us -> 115 us
  between operations: 0.38 us -> 13.9 us
    psum x1 -> x0, blocking collectives: 40.9 us -> none  [per_device(): top_sum = lax.psum(top_partial, 'leaf')]
    gather x27, local copies, waits for them, and re-layouts: 44.5 us -> 17.7 us  [near_step(): other_points = jnp.take(pool_points, column, axis=1)]
    all_gather x1, blocking collectives: 38 us -> 50.3 us  [per_device(): lax.all_gather(base_coeffs.reshape(base_count, K * RHS), 'leaf', axis=0,...]
  transfers between devices with their start and end apart: 6 -> 7, of which waited for: 0 -> 0; matrix products, arithmetic and copies ran while one was open for 10% -> 74% of each run, Pallas kernels for 0% -> 0%
where the time goes in v1:
time: 748 us; the launch traced here: 744 us
  other arithmetic  249 us (33%)
  matrix products  189 us (25%)
  local copies, waits for them, and re-layouts  151 us (20%)
  blocking collectives  115 us (15%)
  starting transfers between devices  24 us (3%)
  between operations  13.9 us (2%)
    dot_general x27, matrix products, near_step(): jnp.einsum('lab,lbr->lar', kernel, other_charges, preferred_element_type=...  175 us
    reduce_sum x27, other arithmetic, near_step(): jnp.sum((points[:, :, :, None] - other_points[:, :, None, :]) ** 2, axis=0)  164 us
    gather x27, local copies, waits for them, and re-layouts, near_step(): other_charges = jnp.take(pool_charges, column, axis=0)  101 us
    all_gather x1, blocking collectives, per_device(): lax.all_gather(lifted.reshape(base_count, K * RHS), 'leaf', axis=0, tiled...  65.2 us
    all_gather x1, blocking collectives, per_device(): lax.all_gather(base_coeffs.reshape(base_count, K * RHS), 'leaf', axis=0,...  50.3 us
    scatter-add x1, other arithmetic, per_device(): jax.ops.segment_sum(results.reshape(-1, K, RHS), local_ids, num_segments=...  31.1 us
    select_n x54, other arithmetic, near_step(): other_points = jnp.take(pool_points, column, axis=1)  22.4 us
    and x27, other arithmetic, near_step(): other_points = jnp.take(pool_points, column, axis=1)  19 us
  transfers between devices with their start and end apart: 7, of which 0 were waited for; matrix products, arithmetic and copies ran while one was open for 74% of the time, Pallas kernels for 0%

profile of v1, /device:TPU:0, one launch (start us, length us, event | category | flops | bytes accessed | tf_op | source)
XLA Modules:
  0.0 744.0 jit_solution(6390165756912751210)
XLA Ops:
  18.7 5.8 collective-permute-start.2
  27.5 8.4 %all-to-all-start = ((s32[32,1,11]{2,1,0:T(1,128)}), s32[32,1,11]{2,1,0:T(1,128)S(1)}, u32[]{:S(2)}, u32[]{:S(2)}) async-start(s32[32,1,11]{2,1,0:T(1,128)} %bitcast.23), calls=%async_computation | async-start | bytes 32768 | tf_op jit(solution)/shard_map/all_to_all | solution.py:128
  39.9 65.2 %all-gather.1 = bf16[32,1,4096]{2,1,0:T(2,128)(2,1)S(1)} all-gather(bf16[1,1,4096]{2,1,0:T(2,128)(2,1)S(1)} %reshape.359), channel_id=1, replica_groups=mesh['leaf'=32] {'leaf'}, dimensions={0}, use_global_device_ids=true | all-gather | bytes 270336 | tf_op jit(solution)/shard_map/all_gather | solution.py:98
  119.3 50.3 %all-gather.2 = bf16[32,1,4096]{2,1,0:T(2,128)(2,1)S(1)} all-gather(bf16[1,1,4096]{2,1,0:T(2,128)(2,1)S(1)} %reshape.361), channel_id=1, replica_groups=mesh['leaf'=32] {'leaf'}, dimensions={0}, use_global_device_ids=true | all-gather | bytes 270336 | tf_op jit(solution)/shard_map/all_gather | solution.py:97
  178.3 4.7 reshape.374
  183.0 6.2 fusion.10
  193.5 5.1 pad_maximum_fusion
  198.7 500.9 %while.12 = (s32[]{:T(128)}, f32[64,128,128]{2,1,0:T(8,128)}, f32[3,8192]{1,0:T(4,128)S(1)}, s32[27,64]{1,0:T(8,128)}, f32[3,192,128]{2,0,1:T(4,128)S(1)}, /*ind...) while((s32[]{:T(128)}, f32[64,128,128]{2,1,0:T(8,128)}, f32[3,8192]{1,0:T(4,128)S(1)}, ...), condition=%wide.region_2.3_spmd.clone, body=%wide.region_0.2_spmd.clone.sunk | while | flops 283141696 | bytes 24057648 | solution.py:41
  200.9 6.1 multiply_reduce_fusion.2
  210.7 5.2 select_add_fusion.2
  218.2 6.1 multiply_reduce_fusion.2
  228.1 6.5 select_add_fusion.2
  236.8 6.1 multiply_reduce_fusion.2
  246.7 6.5 select_add_fusion.2
  255.4 6.1 multiply_reduce_fusion.2
  265.2 6.5 select_add_fusion.2
  274.0 6.1 multiply_reduce_fusion.2
  283.8 6.5 select_add_fusion.2
  292.6 6.1 multiply_reduce_fusion.2
  302.4 6.5 select_add_fusion.2
  311.2 6.1 multiply_reduce_fusion.2
  321.0 6.5 select_add_fusion.2
  329.8 6.1 multiply_reduce_fusion.2
  339.6 6.5 select_add_fusion.2
  348.4 6.1 multiply_reduce_fusion.2
  358.2 6.5 select_add_fusion.2
  367.0 6.1 multiply_reduce_fusion.2
  376.8 6.5 select_add_fusion.2
  385.6 6.1 multiply_reduce_fusion.2
  395.4 6.5 select_add_fusion.2
  404.2 6.1 multiply_reduce_fusion.2
  414.0 6.5 select_add_fusion.2
  422.8 6.1 multiply_reduce_fusion.2
  432.6 6.5 select_add_fusion.2
  441.4 6.1 multiply_reduce_fusion.2
  451.2 6.5 select_add_fusion.2
  460.0 6.1 multiply_reduce_fusion.2
  469.8 6.5 select_add_fusion.2
  478.6 6.1 multiply_reduce_fusion.2
  488.4 6.5 select_add_fusion.2
  497.2 6.1 multiply_reduce_fusion.2
  507.0 6.5 select_add_fusion.2
  515.8 6.1 multiply_reduce_fusion.2
  525.6 6.5 select_add_fusion.2
  534.4 6.1 multiply_reduce_fusion.2
  544.2 6.5 select_add_fusion.2
  553.0 6.1 multiply_reduce_fusion.2
  562.8 6.5 select_add_fusion.2
  571.6 6.1 multiply_reduce_fusion.2
  581.4 6.5 select_add_fusion.2
  590.2 6.1 multiply_reduce_fusion.2
  600.0 6.5 select_add_fusion.2
  608.8 6.1 multiply_reduce_fusion.2
  618.6 6.5 select_add_fusion.2
  627.4 6.1 multiply_reduce_fusion.2
  637.2 6.5 select_add_fusion.2
  646.0 6.1 multiply_reduce_fusion.2
  655.8 6.5 select_add_fusion.2
  664.6 6.1 multiply_reduce_fusion.2
  674.4 6.5 select_add_fusion.2
  683.2 6.1 multiply_reduce_fusion.2
  693.0 6.5 select_add_fusion.2
  701.4 31.1 %scatter_fusion.1 = f32[32,128,1]{1,0,2:T(8,128)S(1)} fusion(f32[32,128,1]{1,0,2:T(8,128)S(1)} %convolution_bitcast_fusion.2, s32[352]{0:T(512)S(1)} %reshape.355, f32[352,32,128]{2,1,0:T(8,128)} %bitcast.137), kind=kCustom, calls=%fused_computation.7 | custom fusion | flops 1441792 | bytes 17302912 | tf_op jit(solution)/shard_map/scatter-add | solution.py:138
  732.8 4.4 fusion.9
  (316 shorter events, 208.5 us)
Async XLA Ops:
  6.5 18.0 %copy-start.11 = (s32[189,1]{0,1:T(1,128)S(1)}, s32[189,1]{0,1:T(1,128)}, u32[]{:S(2)}) copy-start(s32[189,1]{0,1:T(1,128)} %param.23) | copy-start | bytes 2272
  6.5 29.5 %copy-start.8 = (bf16[64,4096]{1,0:T(8,128)(2,1)S(1)}, bf16[64,4096]{1,0:T(8,128)(2,1)}, u32[]{:S(2)}) copy-start(bf16[64,4096]{1,0:T(8,128)(2,1)} %param.18) | copy-start | bytes 1572868
  6.5 29.6 %copy-start.9 = (bf16[8,1024]{1,0:T(8,128)(2,1)S(1)}, bf16[8,1024]{1,0:T(8,128)(2,1)}, u32[]{:S(2)}) copy-start(bf16[8,1024]{1,0:T(8,128)(2,1)} %param.20) | copy-start | bytes 49156
  6.5 29.7 %copy-start.12 = (bf16[1,1024]{1,0:T(2,128)(2,1)S(1)}, bf16[1,1024]{1,0:T(2,128)(2,1)}, u32[]{:S(2)}) copy-start(bf16[1,1024]{1,0:T(2,128)(2,1)} %param.21) | copy-start | bytes 6148
  8.2 28.2 %copy-start.6 = (bf16[64,1024]{1,0:T(8,128)(2,1)S(1)}, bf16[64,1024]{1,0:T(8,128)(2,1)}, u32[]{:S(2)}) copy-start(bf16[64,1024]{1,0:T(8,128)(2,1)} %param.19) | copy-start | bytes 393220
  8.2 28.6 %copy-start = (bf16[8192,128]{1,0:T(8,128)(2,1)S(1)}, bf16[8192,128]{1,0:T(8,128)(2,1)}, u32[]{:S(2)}) copy-start(bf16[8192,128]{1,0:T(8,128)(2,1)} %param.16) | copy-start | bytes 6291460
  8.2 168.1 %collective-permute-start.1 = (f32[64,384]{1,0:T(8,128)}, f32[64,384]{1,0:T(8,128)}, u32[]{:S(2)}, u32[]{:S(2)}) collective-permute-start(f32[64,384]{1,0:T(8,128)} %bitcast.123), channel_id=1, source_target_pairs={{1,0},{2,1},{3,2},{4,3},{5,4},{6,5},{7,6},{8,7},{9,8},{10,9},{11,1... | collective-permute-start | bytes 294920 | tf_op jit(solution)/shard_map/ppermute | solution.py:22
  9.6 167.6 %collective-permute-start = (f32[64,384]{1,0:T(8,128)}, f32[64,384]{1,0:T(8,128)}, u32[]{:S(2)}, u32[]{:S(2)}) collective-permute-start(f32[64,384]{1,0:T(8,128)} %bitcast.123), channel_id=1, source_target_pairs={{0,1},{1,2},{2,3},{3,4},{4,5},{5,6},{6,7},{7,8},{8,9},{9,10},{10,1... | collective-permute-start | bytes 294920 | tf_op jit(solution)/shard_map/ppermute | solution.py:21
  17.4 171.8 %collective-permute-start.3 = (bf16[64,16384]{1,0:T(8,128)(2,1)}, bf16[64,16384]{1,0:T(8,128)(2,1)}, u32[]{:S(2)}, u32[]{:S(2)}) collective-permute-start(bf16[64,16384]{1,0:T(8,128)(2,1)} %reshape_reshape.3), channel_id=1, source_target_pairs={{1,0},{2,1},{3,2},{4,3},{5,4},{6,5},{7,6},{8,7},{9,8},{10,9},{11,1... | collective-permute-start | bytes 6291464 | tf_op jit(solution)/shard_map/ppermute | solution.py:22
  18.7 172.7 %collective-permute-start.2 = (bf16[64,16384]{1,0:T(8,128)(2,1)}, bf16[64,16384]{1,0:T(8,128)(2,1)}, u32[]{:S(2)}, u32[]{:S(2)}) collective-permute-start(bf16[64,16384]{1,0:T(8,128)(2,1)} %reshape_reshape.3), channel_id=1, source_target_pairs={{0,1},{1,2},{2,3},{3,4},{4,5},{5,6},{6,7},{7,8},{8,9},{9,10},{10,1... | collective-permute-start | bytes 6291464 | tf_op jit(solution)/shard_map/ppermute | solution.py:21
  27.5 84.1 %all-to-all-start = ((s32[32,1,11]{2,1,0:T(1,128)}), s32[32,1,11]{2,1,0:T(1,128)S(1)}, u32[]{:S(2)}, u32[]{:S(2)}) async-start(s32[32,1,11]{2,1,0:T(1,128)} %bitcast.23), calls=%async_computation | async-start | bytes 32768 | tf_op jit(solution)/shard_map/all_to_all | solution.py:128
  36.2 70.3 %copy-start.4 = (bf16[8,32,32]{2,1,0:T(8,128)(2,1)}, bf16[8,32,32]{2,1,0:T(8,128)(2,1)S(1)}, u32[]{:S(2)}) copy-start(bf16[8,32,32]{2,1,0:T(8,128)(2,1)S(1)} %reshape.231) | copy-start | bytes 49156
  36.7 69.9 %copy-start.14 = (s32[8]{0:T(128)S(1)}, s32[8]{0:T(128)}, u32[]{:S(2)}) copy-start(s32[8]{0:T(128)} %param.27) | copy-start | bytes 100
  105.0 10.1 %copy-start.10 = (bf16[8,1024]{1,0:T(8,128)(2,1)S(1)}, bf16[8,1024]{1,0:T(8,128)(2,1)}, u32[]{:S(2)}) copy-start(bf16[8,1024]{1,0:T(8,128)(2,1)} %param.25) | copy-start | bytes 49156
  106.6 9.5 %copy-start.13 = (s32[8]{0:T(128)S(1)}, s32[8]{0:T(128)}, u32[]{:S(2)}) copy-start(s32[8]{0:T(128)} %param.26) | copy-start | bytes 100
  109.4 8.1 %copy-start.7 = (bf16[64,1024]{1,0:T(8,128)(2,1)S(1)}, bf16[64,1024]{1,0:T(8,128)(2,1)}, u32[]{:S(2)}) copy-start(bf16[64,1024]{1,0:T(8,128)(2,1)} %param.19) | copy-start | bytes 393220
  111.7 66.6 %all-to-all-start.1 = ((bf16[32,11,1024]{2,1,0:T(8,128)(2,1)}), bf16[32,11,1024]{2,1,0:T(8,128)(2,1)}, u32[]{:S(2)}, u32[]{:S(2)}) async-start(bf16[32,11,1024]{2,1,0:T(8,128)(2,1)} %reshape.239), calls=%async_computation.1 | async-start | bytes 2097152 | tf_op jit(solution)/shard_map/all_to_all | solution.py:127
  115.0 584.5 %all-gather.5.cloned.1.call-start = ((), (), s32[]{:S(2)}) async-start(), calls=%async_computation.2 | async-start | bytes 2162688 | tf_op jit(solution)/shard_map/all_gather | solution.py:113
  116.9 0.6 copy-start.1
  173.2 5.0 copy-start.2
  701.4 31.1 %copy-start.5 = (bf16[8,32,32]{2,1,0:T(8,128)(2,1)S(1)}, bf16[8,32,32]{2,1,0:T(8,128)(2,1)}, u32[]{:S(2)}) copy-start(bf16[8,32,32]{2,1,0:T(8,128)(2,1)} %copy-done.4) | copy-start | bytes 49156
  701.4 31.3 %copy-start.3 = (bf16[64,32,32]{2,1,0:T(8,128)(2,1)S(1)}, bf16[64,32,32]{2,1,0:T(8,128)(2,1)}, u32[]{:S(2)}) copy-start(bf16[64,32,32]{2,1,0:T(8,128)(2,1)} %copy.43) | copy-start | bytes 393220
Sparse Core Ops, SparseCore 0:
  118.7 58.9 all-gather.4
